TPU v7x, 32 devices: a whole 2x2x4 slice. The times are simulated.
32 devices in a mesh: seq: 8 (over z, x), tp: 4 (over y, core).
Axes of the slice: x: 2, y: 2, z: 4, core: 2. Of those that a mesh axis runs over, the one named last changes fastest.
Arguments:
- queries: bfloat16 [1536, 6144], P('seq', 'tp'), may hold values from -400 to 400
- key_vectors: bfloat16 [1536, 1024], P('seq', 'tp'), may hold values from -8 to 8
- value_vectors: bfloat16 [1536, 1024], P('seq', 'tp'), may hold values from -6 to 6
- positions: int32 [1536], P('seq'), may hold values from 0 to 1535, as said below
- residual: bfloat16 [1536, 6144], P('seq', 'tp'), may hold values from -200 to 200
- norm_gain: float32 [1, 6144], P(None, 'tp'), may hold values from 0.5 to 1.5
- out_weight: bfloat16 [6144, 6144], P('tp'), may hold values from -0.3125 to 0.3125
Outputs:
- quantized: bfloat16 [1536, 6144], P('seq')
- token_scale: float32 [1536], P('seq')
- new_residual: bfloat16 [1536, 6144], P('seq', 'tp')
Inputs may be any that keep to these rules, and one draw needn't show every extreme that they name: The positions are a permutation of 0 to 1535. Cut into 16 runs of 96 consecutive positions, the rows of one index of seq hold run r in their first 96 rows and run 2 * 8 - 1 - r in their last ones, both in increasing order, with r differing between the indices of seq.
All inputs are finite; a program needn't handle non-finite values. Where the computation divides by a largest or mean magnitude, that divisor is 1e-20 or more.
Results may differ from a plain program's by a relative error of at most 0.012.
Values may be sent and summed in bfloat16 or wider, within the bound.
A program may use at most 64 MiB of HBM per device.

v0:
```python
import math
import jax
import jax.numpy as jnp
from jax import lax
from jax.sharding import PartitionSpec as P

D = 6144
Q_HEADS = 48
KV_HEADS = 8
HEAD = 128
NEG_FILL = -1e30


def fresh_state(kv_count, state_rows):
    return (
        jnp.full((kv_count, state_rows), NEG_FILL, jnp.float32),
        jnp.zeros((kv_count, state_rows), jnp.float32),
        jnp.zeros((kv_count, state_rows, HEAD), jnp.float32),
    )


def attend(state_now, query_part, half_rows_pos, key_block, value_block, key_pos):
    running_max, running_sum, weighted_sum = state_now
    kv_count = query_part.shape[0]
    group_size = Q_HEADS // KV_HEADS
    score_scale = 1.0 / math.sqrt(HEAD)
    query_pos = jnp.tile(half_rows_pos, group_size)
    key_heads = key_block.reshape(key_block.shape[0], kv_count, HEAD)
    value_heads = value_block.reshape(value_block.shape[0], kv_count, HEAD)
    scores = (
        jnp.einsum("kmd,skd->kms", query_part, key_heads, preferred_element_type=jnp.float32)
        * score_scale
    )
    visible = key_pos[None, :] <= query_pos[:, None]
    scores = jnp.where(visible[None], scores, NEG_FILL)
    new_max = jnp.maximum(running_max, jnp.max(scores, axis=2))
    weights = jnp.where(visible[None], jnp.exp(scores - new_max[..., None]), 0.0)
    factor = jnp.exp(running_max - new_max)
    running_sum = running_sum * factor + jnp.sum(weights, axis=2)
    weighted_sum = weighted_sum * factor[..., None] + jnp.einsum(
        "kms,skd->kmd",
        weights.astype(jnp.bfloat16),
        value_heads,
        preferred_element_type=jnp.float32,
    )
    return (new_max, running_sum, weighted_sum)


def fold_block(states, halves, half_pos, key_block, value_block, key_pos):
    result = []
    for half_index in range(2):

        def compute(state_now, half_index=half_index):
            return attend(
                state_now, halves[half_index], half_pos[half_index], key_block, value_block, key_pos
            )

        result.append(compute(states[half_index]))
    return tuple(result)


def fold_piece(states, halves, half_pos, key_piece, value_piece, key_pos):
    row_count = key_piece.shape[0]
    block_rows = math.gcd(row_count, 1024)
    block_count = row_count // block_rows

    def scan_step(loop_carry, block_pair):
        return (
            fold_block(loop_carry, halves, half_pos, block_pair[0], block_pair[1], block_pair[2]),
            None,
        )

    stacked = (
        key_piece.reshape(block_count, block_rows, key_piece.shape[1]),
        value_piece.reshape(block_count, block_rows, value_piece.shape[1]),
        key_pos.reshape(block_count, block_rows),
    )
    states, unused = lax.scan(scan_step, states, stacked)
    return states


def on_device(queries, key_vectors, value_vectors, positions, residual, norm_gain, out_weight):
    token_rows = queries.shape[0]
    run_rows = token_rows // 2
    group_size = Q_HEADS // KV_HEADS
    kv_count = key_vectors.shape[1] // HEAD
    query_split = queries.reshape(2, run_rows, kv_count, group_size, HEAD).transpose(0, 2, 3, 1, 4)
    query_split = query_split.reshape(2, kv_count, group_size * run_rows, HEAD)
    halves = (query_split[0], query_split[1])
    half_pos = (positions[:run_rows], positions[run_rows:])
    initial = (
        fresh_state(kv_count, group_size * run_rows),
        fresh_state(kv_count, group_size * run_rows),
    )
    all_pos = lax.all_gather(positions, "seq", axis=0, tiled=True)
    kv_pair = jnp.stack((key_vectors, value_vectors))
    pieces = lax.all_gather(kv_pair, "seq", axis=1, tiled=True)
    states = fold_piece(initial, halves, half_pos, pieces[0], pieces[1], all_pos)
    outputs = []
    for state_now in states:
        outputs.append((state_now[2] / state_now[1][..., None]).astype(jnp.bfloat16))
    attended = (
        jnp.stack(outputs).reshape(2, kv_count, group_size, run_rows, HEAD).transpose(0, 3, 1, 2, 4)
    )
    attended = attended.reshape(token_rows, kv_count * group_size * HEAD)
    partial_value = jnp.dot(attended, out_weight, preferred_element_type=jnp.float32)
    partial_value = partial_value.astype(jnp.bfloat16).astype(jnp.float32)
    summed = lax.psum_scatter(
        partial_value.astype(jnp.bfloat16), "tp", scatter_dimension=1, tiled=True
    ).astype(jnp.float32) + residual.astype(jnp.float32)
    square_sum = lax.psum(jnp.sum(summed * summed, axis=1), "tp")
    normed = summed * lax.rsqrt(square_sum / D + 1e-05)[:, None] * norm_gain
    peak_value = lax.pmax(jnp.max(jnp.abs(normed), axis=1), "tp") + 1e-06
    local_scaled = (normed / peak_value[:, None]).astype(jnp.bfloat16)
    quantized = lax.all_gather(local_scaled, "tp", axis=1, tiled=True)
    new_residual = summed.astype(jnp.bfloat16)
    return (quantized, peak_value, new_residual)


def solution(mesh):
    return jax.shard_map(
        on_device,
        mesh=mesh,
        in_specs=(
            P("seq", "tp"),
            P("seq", "tp"),
            P("seq", "tp"),
            P("seq"),
            P("seq", "tp"),
            P(None, "tp"),
            P("tp", None),
        ),
        out_specs=(P("seq", None), P("seq"), P("seq", "tp")),
        check_vma=False,
    )
```

profile of v0, /device:TPU:0, one launch (start us, length us, event | category | flops | bytes accessed | tf_op | source)
XLA Modules:
  0.0 205.4 jit_solution(1911410734703839984)
XLA Ops:
  7.2 1.6 pad_maximum_fusion
  9.0 1.8 reshape.108
  13.3 13.5 %all-reduce = s32[1536]{0:T(1024)S(1)} all-reduce(s32[1536]{0:T(1024)S(1)} %dynamic-update-slice), channel_id=1, replica_groups=mesh['seq'=8,'tp'=4] {'seq'}, use_global_device_ids=true, to_apply=%add | all-reduce | flops 1536 | bytes 12288
  28.1 29.7 %all-gather.3.cloned.1.call-done = bf16[2,1536,256]{2,1,0:T(8,128)(2,1)} async-done(((bf16[2,192,256]{2,1,0:T(8,128)(2,1)}), bf16[2,1536,256]{2,1,0:T(8,128)(2,1)}) %all-gather.3.cloned.1.call-update) | async-done | bytes 1572880 | tf_op jit(solution)/shard_map/all_gather | solution.py:97
  57.7 2.6 %fusion.27 = (bf16[1,1536,256]{2,1,0:T(8,128)(2,1)}, bf16[1,1536,256]{2,1,0:T(8,128)(2,1)}) fusion(bf16[2,1536,256]{2,1,0:T(8,128)(2,1)} %all-gather.3.cloned.1.call-done), kind=kLoop, calls=%fused_computation.56 | loop fusion | bytes 3145728 | tf_op jit(solution)/shard_map/slice | solution.py:98
  60.4 48.9 %while.21 = (s32[]{:T(128)}, f32[2,576]{1,0:T(2,128)S(1)}, f32[2,576]{1,0:T(2,128)S(1)}, f32[2,576,128]{2,1,0:T(8,128)}, f32[2,576]{1,0:T(2,128)S(1)}, /*index=5...) while((s32[]{:T(128)}, f32[2,576]{1,0:T(2,128)S(1)}, ...), condition=%wide.region_5.6_spmd.clone, body=%wide.region_0.5_spmd.clone.sunk | while | flops 620801280 | bytes 39185492 | solution.py:78
  62.9 1.0 constant_dynamic-slice_fusion.7
  66.5 1.4 copy-done
  67.8 1.0 fusion.65
  69.4 1.0 constant_dynamic-slice_fusion.8
  71.2 3.5 %convolution_add_fusion.5 = f32[2,576,128]{2,1,0:T(8,128)} fusion(bf16[512,2,128]{0,2,1:T(8,128)(2,1)} %bitcast.79, f32[2,512,576]{1,2,0:T(8,128)} %copy-done, f32[2,576]{1,0:T(2,128)S(1)} %fusion.64, pred[576,512]{1,0:T(8,128)(4,1)S(1)} %get-tuple-element.288, f32[2,576,128]{2,1,0:T(8,128)} %get-tuple-element.318, ...), kind=kOutput, calls=%fused_computation.10.clone.1 | convolution fusion | flops 154386432 | bytes 4105217 | tf_op jit(solution)/shard_map/while/body/eval_jaxpr/kms,skd->kmd/dot_general | solution.py:40
  79.1 1.0 constant_dynamic-slice_fusion.7
  80.9 1.0 fusion.66
  82.6 1.4 copy-done
  84.0 1.0 fusion.65
  85.6 1.0 constant_dynamic-slice_fusion.8
  87.4 3.7 %convolution_add_fusion.5 = f32[2,576,128]{2,1,0:T(8,128)} fusion(bf16[512,2,128]{0,2,1:T(8,128)(2,1)} %bitcast.79, f32[2,512,576]{1,2,0:T(8,128)} %copy-done, f32[2,576]{1,0:T(2,128)S(1)} %fusion.64, pred[576,512]{1,0:T(8,128)(4,1)S(1)} %get-tuple-element.288, f32[2,576,128]{2,1,0:T(8,128)} %get-tuple-element.318, ...), kind=kOutput, calls=%fused_computation.10.clone.1 | convolution fusion | flops 154386432 | bytes 4105217 | tf_op jit(solution)/shard_map/while/body/eval_jaxpr/kms,skd->kmd/dot_general | solution.py:40
  95.5 1.0 constant_dynamic-slice_fusion.7
  99.0 1.4 copy-done
  100.4 1.0 fusion.65
  102.0 1.0 constant_dynamic-slice_fusion.8
  103.8 3.7 %convolution_add_fusion.5 = f32[2,576,128]{2,1,0:T(8,128)} fusion(bf16[512,2,128]{0,2,1:T(8,128)(2,1)} %bitcast.79, f32[2,512,576]{1,2,0:T(8,128)} %copy-done, f32[2,576]{1,0:T(2,128)S(1)} %fusion.64, pred[576,512]{1,0:T(8,128)(4,1)S(1)} %get-tuple-element.288, f32[2,576,128]{2,1,0:T(8,128)} %get-tuple-element.318, ...), kind=kOutput, calls=%fused_computation.10.clone.1 | convolution fusion | flops 154386432 | bytes 4105217 | tf_op jit(solution)/shard_map/while/body/eval_jaxpr/kms,skd->kmd/dot_general | solution.py:40
  109.2 1.6 divide_convert_fusion.1
  112.0 11.6 %convolution_convert_fusion = bf16[192,6144]{1,0:T(8,128)(2,1)} fusion(bf16[192,1536]{1,0:T(8,128)(2,1)S(1)} %reshape.109, bf16[1536,6144]{1,0:T(8,128)(2,1)} %param.15), kind=kOutput, calls=%fused_computation.43 | convolution fusion | flops 3625058304 | bytes 21823488 | tf_op jit(solution)/shard_map/dot_general | solution.py:106
  124.3 30.6 %reduce-scatter.2.cloned.1.call-done = bf16[192,1536]{1,0:T(8,128)(2,1)} async-done(((bf16[192,6144]{1,0:T(8,128)(2,1)}), bf16[192,1536]{1,0:T(8,128)(2,1)}) %reduce-scatter.2.cloned.1.call-update) | async-done | bytes 589840 | tf_op jit(solution)/shard_map/reduce_scatter | solution.py:108
  154.9 1.4 multiply_reduce_fusion
  156.3 5.8 %psum.7 = f32[192]{0:T(256)S(1)} all-reduce(f32[192]{0:T(256)S(1)} %multiply_reduce_fusion), channel_id=1, replica_groups=mesh['seq'=8,'tp'=4] {'tp'}, use_global_device_ids=true, to_apply=%region_8.9 | all-reduce | flops 192 | bytes 1536 | tf_op jit(solution)/shard_map/psum | solution.py:111
  162.1 1.4 abs_reduce_fusion
  163.5 5.7 %pmax.7 = f32[192]{0:T(256)S(1)} all-reduce(f32[192]{0:T(256)S(1)} %abs_reduce_fusion), channel_id=1, replica_groups=mesh['seq'=8,'tp'=4] {'tp'}, use_global_device_ids=true, to_apply=%region_10.11 | all-reduce | flops 192 | bytes 1536 | tf_op jit(solution)/shard_map/pmax | solution.py:113
  169.2 1.3 fusion.26
  170.5 25.0 %all-gather.5.cloned.1.call-done = bf16[192,6144]{1,0:T(8,128)(2,1)} async-done(((bf16[192,1536]{1,0:T(8,128)(2,1)}), bf16[192,6144]{1,0:T(8,128)(2,1)}) %all-gather.5.cloned.1.call-update) | async-done | bytes 2359312 | tf_op jit(solution)/shard_map/all_gather | solution.py:115
  195.5 3.3 %copy.60 = bf16[192,6144]{1,0:T(8,128)(2,1)} copy(bf16[192,6144]{1,0:T(8,128)(2,1)} %all-gather.5.cloned.1.call-done) | data formatting | bytes 4718592
  (122 shorter events, 28.9 us)
Async XLA Ops:
  7.2 50.6 %all-gather.3.cloned.1.call-start = ((), (), s32[]{:S(2)}) async-start(), calls=%async_computation.1 | async-start | bytes 1769472 | tf_op jit(solution)/shard_map/all_gather | solution.py:97
  8.8 2.9 %copy-start.11 = (u32[32]{0:T(128)S(1)}, u32[32]{0:T(128)}, u32[]{:S(2)}) copy-start(u32[32]{0:T(128)} %constant.37) | copy-start | bytes 388
  8.9 4.2 %copy-start.10 = (s32[192]{0:T(256)S(1)}, s32[192]{0:T(256)}, u32[]{:S(2)}) copy-start(s32[192]{0:T(256)} %param.12) | copy-start | bytes 2308
  8.9 146.0 %reduce-scatter.2.cloned.1.call-start = ((), (), s32[]{:S(2)}) async-start(), calls=%async_computation.2 | async-start | bytes 2949120 | tf_op jit(solution)/shard_map/reduce_scatter | solution.py:108
  64.8 1.0 copy-start.1
  66.4 1.4 copy-start
  71.2 3.5 %copy-start.2 = (bf16[1,512,256]{1,2,0:T(8,128)(2,1)S(1)}, bf16[1,512,256]{1,2,0:T(8,128)(2,1)}, u32[]{:S(2)}) copy-start(bf16[1,512,256]{1,2,0:T(8,128)(2,1)} %copy.36) | copy-start | bytes 786436 | tf_op jit(solution)/shard_map/while
  71.2 3.5 %copy-start.5 = (f32[2,576,128]{2,1,0:T(8,128)S(1)}, f32[2,576,128]{2,1,0:T(8,128)}, u32[]{:S(2)}) copy-start(f32[2,576,128]{2,1,0:T(8,128)} %get-tuple-element.315) | copy-start | bytes 1769476 | tf_op jit(solution)/shard_map/while
  71.2 3.5 %copy-start.7 = (f32[2,576]{1,0:T(2,128)S(1)}, f32[2,576]{1,0:T(2,128)}, u32[]{:S(2)}) copy-start(f32[2,576]{1,0:T(2,128)} %get-tuple-element.293) | copy-start | bytes 13828 | tf_op jit(solution)/shard_map/while
  75.7 0.8 copy-start.6
  80.9 1.0 copy-start.1
  82.6 1.4 copy-start
  87.4 3.7 %copy-start.2 = (bf16[1,512,256]{1,2,0:T(8,128)(2,1)S(1)}, bf16[1,512,256]{1,2,0:T(8,128)(2,1)}, u32[]{:S(2)}) copy-start(bf16[1,512,256]{1,2,0:T(8,128)(2,1)} %copy.36) | copy-start | bytes 786436 | tf_op jit(solution)/shard_map/while
  87.4 3.7 %copy-start.5 = (f32[2,576,128]{2,1,0:T(8,128)S(1)}, f32[2,576,128]{2,1,0:T(8,128)}, u32[]{:S(2)}) copy-start(f32[2,576,128]{2,1,0:T(8,128)} %get-tuple-element.315) | copy-start | bytes 1769476 | tf_op jit(solution)/shard_map/while
  87.4 3.7 %copy-start.7 = (f32[2,576]{1,0:T(2,128)S(1)}, f32[2,576]{1,0:T(2,128)}, u32[]{:S(2)}) copy-start(f32[2,576]{1,0:T(2,128)} %get-tuple-element.293) | copy-start | bytes 13828 | tf_op jit(solution)/shard_map/while
  92.1 0.8 copy-start.6
  97.3 1.0 copy-start.1
  98.9 1.4 copy-start
  103.8 3.7 %copy-start.2 = (bf16[1,512,256]{1,2,0:T(8,128)(2,1)S(1)}, bf16[1,512,256]{1,2,0:T(8,128)(2,1)}, u32[]{:S(2)}) copy-start(bf16[1,512,256]{1,2,0:T(8,128)(2,1)} %copy.36) | copy-start | bytes 786436 | tf_op jit(solution)/shard_map/while
  103.8 3.7 %copy-start.5 = (f32[2,576,128]{2,1,0:T(8,128)S(1)}, f32[2,576,128]{2,1,0:T(8,128)}, u32[]{:S(2)}) copy-start(f32[2,576,128]{2,1,0:T(8,128)} %get-tuple-element.315) | copy-start | bytes 1769476 | tf_op jit(solution)/shard_map/while
  103.8 3.7 %copy-start.7 = (f32[2,576]{1,0:T(2,128)S(1)}, f32[2,576]{1,0:T(2,128)}, u32[]{:S(2)}) copy-start(f32[2,576]{1,0:T(2,128)} %get-tuple-element.293) | copy-start | bytes 13828 | tf_op jit(solution)/shard_map/while
  108.4 0.8 copy-start.6
  123.6 0.7 copy-start.8
  123.6 31.3 %copy-start.3 = (bf16[192,1536]{1,0:T(8,128)(2,1)S(1)}, bf16[192,1536]{1,0:T(8,128)(2,1)}, u32[]{:S(2)}) copy-start(bf16[192,1536]{1,0:T(8,128)(2,1)} %param.13) | copy-start | bytes 1769476
  123.6 71.9 %all-gather.5.cloned.1.call-start = ((), (), s32[]{:S(2)}) async-start(), calls=%async_computation.3 | async-start | bytes 2949120 | tf_op jit(solution)/shard_map/all_gather | solution.py:115
  154.9 14.3 %copy-start.4 = (bf16[192,1536]{1,0:T(8,128)(2,1)S(1)}, bf16[192,1536]{1,0:T(8,128)(2,1)}, u32[]{:S(2)}) copy-start(bf16[192,1536]{1,0:T(8,128)(2,1)} %reduce-scatter.2.cloned.1.call-done) | copy-start | bytes 1769476
  169.2 29.7 %copy-start.9 = (f32[192]{0:T(256)}, f32[192]{0:T(256)S(1)}, u32[]{:S(2)}) copy-start(f32[192]{0:T(256)S(1)} %broadcast_add_fusion) | copy-start | bytes 2308
Sparse Core Ops, SparseCore 0:
  10.7 46.9 all-gather.2
  123.7 31.1 reduce-scatter.1
  170.6 24.8 all-gather.4
where the time goes:
time: 206 us; the launch traced here: 205 us
  waiting for transfers between devices  85.3 us (41%)
  local copies, waits for them, and re-layouts  34.3 us (17%)
  matrix products  29.4 us (14%)
  blocking collectives  24.9 us (12%)
  other arithmetic  16.5 us (8%)
  between operations  14.5 us (7%)
    reduce_scatter x1, waiting for transfers between devices, on_device(): lax.psum_scatter(partial_value.astype(jnp.bfloat16), 'tp', scatter_dimens...  30.6 us
    all_gather x1, waiting for transfers between devices, on_device(): pieces = lax.all_gather(kv_pair, 'seq', axis=1, tiled=True)  29.7 us
    all_gather x1, waiting for transfers between devices, on_device(): quantized = lax.all_gather(local_scaled, 'tp', axis=1, tiled=True)  25 us
    dot_general x6, matrix products, attend(): jnp.einsum('kms,skd->kmd', weights.astype(jnp.bfloat16), value_heads, pre...  13.7 us
    unnamed x1, blocking collectives  13.5 us
    dot_general x1, matrix products, on_device(): jnp.dot(attended, out_weight, preferred_element_type=jnp.float32)  11.6 us
    dynamic_slice x15, local copies, waits for them, and re-layouts, fold_piece(): states, unused = lax.scan(scan_step, states, stacked)  10.9 us
    while x42, local copies, waits for them, and re-layouts  6.63 us
  transfers between devices with their start and end apart: 3, of which 3 were waited for; matrix products, arithmetic and copies ran while one was open for 2% of the time, Pallas kernels for 0%

commit v1 on v0

--- a/solution.py
+++ b/solution.py
@@ -112,7 +112,16 @@
     normed = summed * lax.rsqrt(square_sum / D + 1e-05)[:, None] * norm_gain
     peak_value = lax.pmax(jnp.max(jnp.abs(normed), axis=1), "tp") + 1e-06
     local_scaled = (normed / peak_value[:, None]).astype(jnp.bfloat16)
-    quantized = lax.all_gather(local_scaled, "tp", axis=1, tiled=True)
+    axis_len = jax.lax.psum(1, "tp")
+    z2 = [(at - 1, at) for at in range(1, axis_len)] + [(axis_len - 1, 0)]
+    t1 = local_scaled
+    kept_rows = [t1]
+    for _ in tuple(range(axis_len - 1)):
+        t1 = jax.lax.ppermute(t1, "tp", z2)
+        kept_rows += [t1]
+    k_now = jnp.concatenate([*reversed(kept_rows)], axis=1)
+    val = jax.lax.axis_index("tp")
+    quantized = jnp.roll(k_now, (val + 1) * t1.shape[1], axis=1)
     new_residual = summed.astype(jnp.bfloat16)
     return (quantized, peak_value, new_residual)
 

time: 206 us -> 193 us (0.937)
  matrix products: 29.4 us -> 21.5 us
  local copies, waits for them, and re-layouts: 34.3 us -> 26.5 us
  waiting for transfers between devices: 85.3 us -> 87.7 us
    ppermute x0 -> x3, waiting for transfers between devices: none -> 27.9 us  [on_device(): t1 = jax.lax.ppermute(t1, 'tp', z2)]
    all_gather x1 -> x0, waiting for transfers between devices: 25 us -> none  [on_device(): quantized = lax.all_gather(local_scaled, 'tp', axis=1, tiled=True)]
    dot_general x6, matrix products: 13.7 us -> 5.82 us  [attend(): jnp.einsum('kms,skd->kmd', weights.astype(jnp.bfloat16), value_heads, pre...]
    dynamic_slice x15, local copies, waits for them, and re-layouts: 10.9 us -> 4.84 us  [fold_piece(): states, unused = lax.scan(scan_step, states, stacked)]
    while x42, local copies, waits for them, and re-layouts: 6.63 us -> 2.63 us
    le x6, local copies, waits for them, and re-layouts: 0.45 us -> 4.01 us  [attend(): visible = key_pos[None, :] <= query_pos[:, None]]
    dynamic_slice x0 -> x1, local copies, waits for them, and re-layouts: none -> 2.27 us  [on_device(): quantized = jnp.roll(k_now, (val + 1) * t1.shape[1], axis=1)]
    le x3, other arithmetic: 1.2 us -> 3.3 us  [attend(): visible = key_pos[None, :] <= query_pos[:, None]]
  transfers between devices with their start and end apart: 3 -> 5, of which waited for: 3 -> 5; matrix products, arithmetic and copies ran while one was open for 2% -> 3% of each run, Pallas kernels for 0% -> 0%
where the time goes in v1:
time: 193 us; the launch traced here: 192 us
  waiting for transfers between devices  87.7 us (45%)
  local copies, waits for them, and re-layouts  26.5 us (14%)
  blocking collectives  24.8 us (13%)
  matrix products  21.5 us (11%)
  other arithmetic  16.5 us (9%)
  between operations  14.9 us (8%)
    reduce_scatter x1, waiting for transfers between devices, on_device(): lax.psum_scatter(partial_value.astype(jnp.bfloat16), 'tp', scatter_dimens...  30.6 us
    all_gather x1, waiting for transfers between devices, on_device(): pieces = lax.all_gather(kv_pair, 'seq', axis=1, tiled=True)  29.2 us
    ppermute x3, waiting for transfers between devices, on_device(): t1 = jax.lax.ppermute(t1, 'tp', z2)  27.9 us
    unnamed x1, blocking collectives  13.3 us
    dot_general x1, matrix products, on_device(): jnp.dot(attended, out_weight, preferred_element_type=jnp.float32)  11.6 us
    reduce_sum x6, other arithmetic, attend(): running_sum = running_sum * factor + jnp.sum(weights, axis=2)  5.85 us
    dot_general x6, matrix products, attend(): jnp.einsum('kms,skd->kmd', weights.astype(jnp.bfloat16), value_heads, pre...  5.82 us
    psum x1, blocking collectives, on_device(): square_sum = lax.psum(jnp.sum(summed * summed, axis=1), 'tp')  5.75 us
  transfers between devices with their start and end apart: 5, of which 5 were waited for; matrix products, arithmetic and copies ran while one was open for 3% of the time, Pallas kernels for 0%

profile of v1, /device:TPU:0, one launch (start us, length us, event | category | flops | bytes accessed | tf_op | source)
XLA Modules:
  0.0 192.4 jit_solution(11197326863092627866)
XLA Ops:
  7.2 1.6 pad_maximum_fusion
  9.0 1.3 dynamic-slice
  11.8 13.3 %all-reduce = s32[1536]{0:T(1024)S(1)} all-reduce(s32[1536]{0:T(1024)S(1)} %dynamic-update-slice), channel_id=1, replica_groups=mesh['seq'=8,'tp'=4] {'seq'}, use_global_device_ids=true, to_apply=%add | all-reduce | flops 1536 | bytes 12288
  25.7 1.8 reshape.108
  28.5 29.2 %all-gather.2.cloned.1.call-done = bf16[2,1536,256]{2,1,0:T(8,128)(2,1)} async-done(((bf16[2,192,256]{2,1,0:T(8,128)(2,1)}), bf16[2,1536,256]{2,1,0:T(8,128)(2,1)}) %all-gather.2.cloned.1.call-update) | async-done | bytes 1572880 | tf_op jit(solution)/shard_map/all_gather | solution.py:97
  57.7 1.5 fusion.27
  59.1 34.9 %while.21 = (s32[]{:T(128)}, f32[2,576]{1,0:T(2,128)S(1)}, f32[2,576]{1,0:T(2,128)}, f32[2,576,128]{2,1,0:T(8,128)}, f32[2,576]{1,0:T(2,128)S(1)}, /*index=5*/f3...) while((s32[]{:T(128)}, f32[2,576]{1,0:T(2,128)S(1)}, ...), condition=%wide.region_5.6_spmd.clone, body=%wide.region_0.5_spmd.clone.sunk | while | flops 620801280 | bytes 27575388 | solution.py:78
  59.2 1.3 constant_dynamic-slice_fusion.7
  63.4 1.1 broadcast_compare_fusion.3
  65.2 1.0 fusion.66
  69.0 1.0 convolution_add_fusion.4
  70.8 1.3 constant_dynamic-slice_fusion.7
  75.0 1.1 broadcast_compare_fusion.3
  76.8 1.0 fusion.66
  78.5 1.0 fusion.65
  80.6 1.0 convolution_add_fusion.4
  82.4 1.3 constant_dynamic-slice_fusion.7
  86.6 1.1 broadcast_compare_fusion.3
  88.4 1.0 fusion.66
  92.2 1.0 convolution_add_fusion.4
  94.0 1.4 divide_convert_fusion.1
  96.6 11.6 %convolution_convert_fusion = bf16[192,6144]{1,0:T(8,128)(2,1)} fusion(bf16[192,1536]{1,0:T(8,128)(2,1)S(1)} %reshape.109, bf16[1536,6144]{1,0:T(8,128)(2,1)} %param.15), kind=kOutput, calls=%fused_computation.43 | convolution fusion | flops 3625058304 | bytes 21823488 | tf_op jit(solution)/shard_map/dot_general | solution.py:106
  108.9 30.6 %reduce-scatter.2.cloned.1.call-done = bf16[192,1536]{1,0:T(8,128)(2,1)} async-done(((bf16[192,6144]{1,0:T(8,128)(2,1)}), bf16[192,1536]{1,0:T(8,128)(2,1)}) %reduce-scatter.2.cloned.1.call-update) | async-done | bytes 589840 | tf_op jit(solution)/shard_map/reduce_scatter | solution.py:108
  139.5 1.4 multiply_reduce_fusion
  140.9 5.8 %psum.7 = f32[192]{0:T(256)S(1)} all-reduce(f32[192]{0:T(256)S(1)} %multiply_reduce_fusion), channel_id=1, replica_groups=mesh['seq'=8,'tp'=4] {'tp'}, use_global_device_ids=true, to_apply=%region_8.9 | all-reduce | flops 192 | bytes 1536 | tf_op jit(solution)/shard_map/psum | solution.py:111
  146.7 1.4 abs_reduce_fusion
  148.1 5.7 %pmax.7 = f32[192]{0:T(256)S(1)} all-reduce(f32[192]{0:T(256)S(1)} %abs_reduce_fusion), channel_id=1, replica_groups=mesh['seq'=8,'tp'=4] {'tp'}, use_global_device_ids=true, to_apply=%region_10.11 | all-reduce | flops 192 | bytes 1536 | tf_op jit(solution)/shard_map/pmax | solution.py:113
  153.8 1.1 fusion.26
  154.9 9.3 %collective-permute-done = bf16[192,1536]{1,0:T(8,128)(2,1)S(1)} collective-permute-done((bf16[192,1536]{1,0:T(8,128)(2,1)S(1)}, bf16[192,1536]{1,0:T(8,128)(2,1)S(1)}, u32[]{:S(2)}, u32[]{:S(2)}) %collective-permute-start) | collective-permute-done | bytes 589856 | tf_op jit(solution)/shard_map/ppermute | solution.py:120
  164.2 9.3 %collective-permute-done.1 = bf16[192,1536]{1,0:T(8,128)(2,1)S(1)} collective-permute-done((bf16[192,1536]{1,0:T(8,128)(2,1)S(1)}, bf16[192,1536]{1,0:T(8,128)(2,1)S(1)}, u32[]{:S(2)}, u32[]{:S(2)}) %collective-permute-start.1) | collective-permute-done | bytes 589856 | tf_op jit(solution)/shard_map/ppermute | solution.py:120
  173.5 9.3 %collective-permute-done.2 = bf16[192,1536]{1,0:T(8,128)(2,1)S(1)} collective-permute-done((bf16[192,1536]{1,0:T(8,128)(2,1)S(1)}, bf16[192,1536]{1,0:T(8,128)(2,1)S(1)}, u32[]{:S(2)}, u32[]{:S(2)}) %collective-permute-start.2) | collective-permute-done | bytes 589856 | tf_op jit(solution)/shard_map/ppermute | solution.py:120
  183.3 2.3 %constant_dynamic-slice_fusion.3 = bf16[192,6144]{1,0:T(8,128)(2,1)} fusion(bf16[192,12288]{1,0:T(8,128)(2,1)S(1)} %constant_dynamic-update-slice_fusion, s32[]{:T(128)S(6)} %select_n.27), kind=kLoop, calls=%fused_computation.64 | loop fusion | bytes 4718596 | tf_op jit(solution)/shard_map/jit(_roll_dynamic)/dynamic_slice | solution.py:124
  (131 shorter events, 25.2 us)
Async XLA Ops:
  7.2 50.5 %all-gather.2.cloned.1.call-start = ((), (), s32[]{:S(2)}) async-start(), calls=%async_computation.1 | async-start | bytes 1769472 | tf_op jit(solution)/shard_map/all_gather | solution.py:97
  8.8 19.0 %copy-start.10 = (s32[192]{0:T(256)S(1)}, s32[192]{0:T(256)}, u32[]{:S(2)}) copy-start(s32[192]{0:T(256)} %param.12) | copy-start | bytes 2308
  8.9 130.6 %reduce-scatter.2.cloned.1.call-start = ((), (), s32[]{:S(2)}) async-start(), calls=%async_computation.2 | async-start | bytes 2949120 | tf_op jit(solution)/shard_map/reduce_scatter | solution.py:108
  66.2 1.7 copy-start.4
  66.2 1.7 copy-start.6
  67.9 1.0 copy-start.5
  67.9 1.0 copy-start.7
  67.9 1.1 copy-start.2
  70.0 0.8 copy-start.3
  77.8 1.7 copy-start.4
  77.8 1.7 copy-start.6
  79.5 1.0 copy-start.5
  79.5 1.0 copy-start.7
  79.5 1.1 copy-start.2
  81.6 0.8 copy-start.3
  89.4 1.7 copy-start.4
  89.4 1.7 copy-start.6
  91.1 1.0 copy-start.5
  91.1 1.0 copy-start.7
  91.1 1.1 copy-start.2
  93.2 0.8 copy-start.3
  108.2 0.7 copy-start.8
  108.2 31.3 %copy-start = (bf16[192,1536]{1,0:T(8,128)(2,1)S(1)}, bf16[192,1536]{1,0:T(8,128)(2,1)}, u32[]{:S(2)}) copy-start(bf16[192,1536]{1,0:T(8,128)(2,1)} %param.13) | copy-start | bytes 1769476
  139.5 14.3 %copy-start.1 = (bf16[192,1536]{1,0:T(8,128)(2,1)S(1)}, bf16[192,1536]{1,0:T(8,128)(2,1)}, u32[]{:S(2)}) copy-start(bf16[192,1536]{1,0:T(8,128)(2,1)} %reduce-scatter.2.cloned.1.call-done) | copy-start | bytes 1769476
  153.8 29.2 %copy-start.9 = (f32[192]{0:T(256)}, f32[192]{0:T(256)S(1)}, u32[]{:S(2)}) copy-start(f32[192]{0:T(256)S(1)} %broadcast_add_fusion) | copy-start | bytes 2308
  154.9 9.3 %collective-permute-start = (bf16[192,1536]{1,0:T(8,128)(2,1)S(1)}, bf16[192,1536]{1,0:T(8,128)(2,1)S(1)}, u32[]{:S(2)}, u32[]{:S(2)}) collective-permute-start(bf16[192,1536]{1,0:T(8,128)(2,1)S(1)} %get-tuple-element.184), channel_id=1, source_target_pairs={{0,1},{1,2},{2,3},{3,0},{4,5},{5,6},{6,7},{7,4},{8,9},{9,10},{10,1... | collective-permute-start | bytes 1769480 | tf_op jit(solution)/shard_map/ppermute | solution.py:120
  164.2 9.3 %collective-permute-start.1 = (bf16[192,1536]{1,0:T(8,128)(2,1)S(1)}, bf16[192,1536]{1,0:T(8,128)(2,1)S(1)}, u32[]{:S(2)}, u32[]{:S(2)}) collective-permute-start(bf16[192,1536]{1,0:T(8,128)(2,1)S(1)} %collective-permute-done), channel_id=1, source_target_pairs={{0,1},{1,2},{2,3},{3,0},{4,5},{5,6},{6,7},{7,4},{8,9},{9,10},{10,1... | collective-permute-start | bytes 1769480 | tf_op jit(solution)/shard_map/ppermute | solution.py:120
  173.5 9.3 %collective-permute-start.2 = (bf16[192,1536]{1,0:T(8,128)(2,1)S(1)}, bf16[192,1536]{1,0:T(8,128)(2,1)S(1)}, u32[]{:S(2)}, u32[]{:S(2)}) collective-permute-start(bf16[192,1536]{1,0:T(8,128)(2,1)S(1)} %collective-permute-done.1), channel_id=1, source_target_pairs={{0,1},{1,2},{2,3},{3,0},{4,5},{5,6},{6,7},{7,4},{8,9},{9,10},{10,1... | collective-permute-start | bytes 1769480 | tf_op jit(solution)/shard_map/ppermute | solution.py:120
Sparse Core Ops, SparseCore 0:
  10.7 46.8 all-gather.1
  108.3 31.1 reduce-scatter.1
